TPU v7x, 256 devices: a whole 4x4x8 slice. The times are simulated.
256 devices in a mesh: tok: 16 (over z, core), vocab: 16 (over y, x).
Axes of the slice: x: 4, y: 4, z: 8, core: 2. Of those that a mesh axis runs over, the one named last changes fastest.
Arguments:
- latent_vectors: float32 [1536, 3584], P('tok'), may hold values from -400 to 400
- unembedding_matrix: float32 [3584, 152064], P(None, ('tok', 'vocab')), may hold values from -0.09375 to 0.09375
- drawn_symbols: int32 [1536], P('tok'), may hold values from 0 to 152063
- piece_extents: int32 [16, 4], P('tok'), may hold values from 1 to 48, 96 in all within a row
- piece_episode_lookup: int32 [16, 4], P('tok'), may hold values from 0 to 1023
- episode_heats: float32 [1024], replicated, may hold values from 0.6 to 1.5
Outputs:
- seg_logprob: float32 [64], P('tok')
Inputs may be any that keep to these rules, and one draw needn't show every extreme that they name: `piece_extents`: each row of lengths sums to 96.
All inputs are finite; a program needn't handle non-finite values.
Results may differ from a plain program's by a relative error of at most 0.0003.
Values sent between devices are 32-bit elements; how exact they have to be, the bound alone decides.
A program may use at most 128 MiB of HBM per device.

v0:
```python
import jax
import jax.numpy as jnp
from jax import lax
from jax.sharding import Mesh
from jax.sharding import PartitionSpec as P

TOK = ("tok_0", "tok_1")
VOCAB = ("vocab_0", "vocab_1")
TOK_VOCAB = ("tok_0", "tok_1", "vocab_0", "vocab_1")


def collected_together(x, axis):
    leaves = jax.tree.leaves(x)
    order = sorted(range(len(leaves)), key=lambda k: -leaves[k].size)
    width = (1, *leaves[order[0]].shape)[-1]
    lines = [
        jnp.pad(leaves[k].reshape(-1), (0, -leaves[k].size % width)).reshape(-1, width)
        for k in order
    ]
    both, at, found = (lax.all_gather(jnp.concatenate(lines), axis), 0, {})
    for k, line in zip(order, lines):
        piece = both[:, at : at + len(line)].reshape(len(both), -1)
        found[k] = piece[:, : leaves[k].size].reshape(-1, *leaves[k].shape)
        at += len(line)
    numbers = iter(range(len(leaves)))
    return jax.tree.map(lambda _: found[next(numbers)], x)


def merged_by_axis(x, axes, combine):
    for axis in axes:
        pieces = collected_together(x, axis)
        x = jax.tree.map(lambda part: part[0], pieces)
        for k in range(1, lax.axis_size(axis)):
            x = combine(x, jax.tree.map(lambda part: part[k], pieces))
    return x


def combine_pairs(earlier, later):
    peak = jnp.maximum(earlier[0], later[0])
    total = earlier[1] * jnp.exp(earlier[0] - peak) + later[1] * jnp.exp(later[0] - peak)
    return (peak, total, earlier[2] + later[2])


def on_device(
    latent_vectors,
    unembedding_matrix,
    drawn_symbols,
    piece_extents,
    piece_episode_lookup,
    episode_heats,
):
    tok_rows = latent_vectors.shape[0]
    ends = jnp.cumsum(piece_extents[0])
    starts = ends - piece_extents[0]
    position = jnp.arange(tok_rows, dtype=jnp.int32)
    piece_episode = (
        (position[None, :] >= starts[:, None]) & (position[None, :] < ends[:, None])
    ).astype(jnp.float32)
    chosen_symbol = (
        piece_episode_lookup[0][:, None]
        == jnp.arange(episode_heats.shape[0], dtype=jnp.int32)[None, :]
    ).astype(jnp.float32)
    piece_reciprocal_heat = jnp.dot(
        chosen_symbol, 1.0 / episode_heats, precision=lax.Precision.HIGHEST
    )
    symbol_reciprocal_heat = jnp.dot(
        piece_reciprocal_heat, piece_episode, precision=lax.Precision.HIGHEST
    )
    gathered, scale_all, target_all = (
        lax.all_gather(latent_vectors, TOK, axis=0, tiled=True),
        lax.all_gather(symbol_reciprocal_heat, TOK, axis=0, tiled=True),
        lax.all_gather(drawn_symbols, TOK, axis=0, tiled=True),
    )
    width = unembedding_matrix.shape[1]
    column_start = (lax.axis_index(TOK) * lax.axis_size(VOCAB) + lax.axis_index(VOCAB)) * width
    logits = (
        jnp.dot(
            gathered,
            unembedding_matrix,
            preferred_element_type=jnp.float32,
            precision=lax.Precision.HIGHEST,
        )
        * scale_all[:, None]
    )
    ids = column_start + jnp.arange(width, dtype=jnp.int32)
    picked = jnp.sum(jnp.where(target_all[:, None] == ids[None, :], logits, 0.0), axis=1)
    local_top = jnp.max(logits, axis=1)
    local_total = jnp.sum(jnp.exp(logits - local_top[:, None]), axis=1)
    top, total, target_logit = merged_by_axis(
        (local_top, local_total, picked), TOK_VOCAB, combine_pairs
    )
    logprob = target_logit - top - jnp.log(total)
    own = lax.dynamic_slice_in_dim(logprob, lax.axis_index(TOK) * tok_rows, tok_rows, 0)
    sums = jnp.dot(piece_episode, own, precision=lax.Precision.HIGHEST)
    return sums / piece_extents[0].astype(jnp.float32)


def solution(mesh):
    finer = Mesh(mesh.devices.reshape(8, 2, 4, 4), ("tok_0", "tok_1", "vocab_0", "vocab_1"))
    return jax.shard_map(
        on_device,
        mesh=finer,
        in_specs=(P(TOK, None), P(None, TOK_VOCAB), P(TOK), P(TOK, None), P(TOK, None), P()),
        out_specs=P(TOK),
        check_vma=False,
    )
```

profile of v0, /device:TPU:2, one launch (start us, length us, event | category | flops | bytes accessed | tf_op | source)
XLA Modules:
  0.0 244.3 jit_solution(13467237366138529779)
XLA Ops:
  6.5 0.0 all-gather.10.cloned.1.call-start
  6.5 0.7 all-gather.10.cloned.1.call-update
  7.3 0.8 reduce-window.7
  8.1 1.3 dynamic-slice
  10.0 0.7 bitcast_subtract_fusion
  10.7 0.7 broadcast_divide_fusion
  11.4 0.8 convolution_bitcast_fusion.2
  12.2 0.2 convolution_bitcast_fusion.1
  12.4 0.2 dynamic-update-slice
  12.6 0.8 dynamic-update-slice.1
  13.5 32.3 %all-reduce = f32[1536]{0:T(1024)S(1)} all-reduce(f32[1536]{0:T(1024)S(1)} %dynamic-update-slice), channel_id=1, replica_groups=mesh['tok_0'=8,'tok_1'=2,'vocab_0'=4,'vocab_1'=4] {'tok_0','tok_1'}, use_global_device_ids=true, to_apply=%add | all-reduce | flops 1536 | bytes 12288
  45.8 10.6 %all-reduce.1 = s32[1536]{0:T(1024)S(1)} all-reduce(s32[1536]{0:T(1024)S(1)} %dynamic-update-slice.1), channel_id=1, replica_groups=mesh['tok_0'=8,'tok_1'=2,'vocab_0'=4,'vocab_1'=4] {'tok_0','tok_1'}, use_global_device_ids=true, to_apply=%add.1 | all-reduce | flops 1536 | bytes 12288
  56.3 76.7 %all-gather.10.cloned.1.call-done = f32[1536,3584]{1,0:T(8,128)} async-done(((f32[96,3584]{1,0:T(8,128)}), f32[1536,3584]{1,0:T(8,128)}) %all-gather.10.cloned.1.call-update) | async-done | bytes 22020112 | tf_op jit(solution)/shard_map/all_gather | solution.py:70
  133.1 51.2 %fusion.65 = (f32[1536]{0:T(1024)S(1)}, f32[1536,594]{0,1:T(8,128)S(1)}) fusion(f32[1536]{0:T(1024)S(1)} %all-reduce, f32[1536,3584]{1,0:T(8,128)} %all-gather.10.cloned.1.call-done, f32[3584,594]{0,1:T(8,128)} %param.7), kind=kOutput, calls=%fused_computation.134 | convolution fusion | flops 39241633792 | bytes 34197504 | tf_op jit(solution)/shard_map/dot_general | solution.py:77
  184.3 0.0 copy-start
  184.3 0.9 exponential_reduce_fusion
  185.2 24.7 %all-gather.4 = f32[8,3,1536]{2,1,0:T(4,128)S(1)} all-gather(f32[1,3,1536]{2,1,0:T(4,128)S(1)} %maximum_bitcast_fusion), channel_id=2, replica_groups=mesh['tok_0'=8,'tok_1'=2,'vocab_0'=4,'vocab_1'=4] {'tok_0'}, dimensions={0}, use_global_device_ids=true | all-gather | bytes 165888 | tf_op jit(solution)/shard_map/all_gather | solution.py:20
  210.0 0.1 fusion.19
  210.2 1.8 all-gather.5
  212.1 12.3 %all-gather.6 = f32[4,3,1536]{2,1,0:T(4,128)S(1)} all-gather(f32[1,3,1536]{2,1,0:T(4,128)S(1)} %maximum_bitcast_fusion.2), channel_id=4, replica_groups=mesh['tok_0'=8,'tok_1'=2,'vocab_0'=4,'vocab_1'=4] {'vocab_0'}, dimensions={0}, use_global_device_ids=true | all-gather | bytes 92160 | tf_op jit(solution)/shard_map/all_gather | solution.py:20
  224.4 0.1 fusion.5
  224.5 11.9 %all-gather.7 = f32[4,3,1536]{2,1,0:T(4,128)S(1)} all-gather(f32[1,3,1536]{2,1,0:T(4,128)S(1)} %maximum_bitcast_fusion.3), channel_id=5, replica_groups=mesh['tok_0'=8,'tok_1'=2,'vocab_0'=4,'vocab_1'=4] {'vocab_1'}, dimensions={0}, use_global_device_ids=true | all-gather | bytes 92160 | tf_op jit(solution)/shard_map/all_gather | solution.py:20
  236.4 0.2 slice_reduce_fusion.3
  236.7 0.0 copy-done
  236.7 0.7 fusion
  (17 shorter events, 0.3 us)
Async XLA Ops:
  6.5 126.5 %all-gather.10.cloned.1.call-start = ((), (), s32[]{:S(2)}) async-start(), calls=%async_computation | async-start | bytes 23396352 | tf_op jit(solution)/shard_map/all_gather | solution.py:70
  184.3 52.4 %copy-start = (s32[1,4]{1,0:T(1,128)S(1)}, s32[1,4]{1,0:T(1,128)}, u32[]{:S(2)}) copy-start(s32[1,4]{1,0:T(1,128)} %param.9) | copy-start | bytes 52
Sparse Core Ops, SparseCore 0:
  9.2 123.8 all-gather.9
where the time goes:
time: 244 us
  blocking collectives  93.6 us (38%)
  waiting for transfers between devices  77.4 us (32%)
  matrix products  53 us (22%)
  between operations  14.2 us (6%)
  other arithmetic  3.67 us (2%)
    all_gather x1, waiting for transfers between devices, on_device(): lax.all_gather(latent_vectors, TOK, axis=0, tiled=True)  76.7 us
    dot_general x1, matrix products, on_device(): jnp.dot(gathered, unembedding_matrix, preferred_element_type=jnp.float32,...  51.2 us
    all_gather x4, blocking collectives, collected_together(): both, at, found = (lax.all_gather(jnp.concatenate(lines), axis), 0, {})  50.7 us
    unnamed x2, blocking collectives  42.8 us
  transfers between devices with their start and end apart: 1, of which 1 were waited for; matrix products, arithmetic and copies ran while one was open for 2% of the time, Pallas kernels for 0%

commit v1 on v0

--- a/solution.py
+++ b/solution.py
@@ -67,7 +67,9 @@
         piece_reciprocal_heat, piece_episode, precision=lax.Precision.HIGHEST
     )
     gathered, scale_all, target_all = (
-        lax.all_gather(latent_vectors, TOK, axis=0, tiled=True),
+        jnp.concatenate(
+            lax.all_to_all(jnp.stack([latent_vectors] * lax.axis_size(TOK)), TOK, 0, 0), axis=0
+        ),
         lax.all_gather(symbol_reciprocal_heat, TOK, axis=0, tiled=True),
         lax.all_gather(drawn_symbols, TOK, axis=0, tiled=True),
     )

time: 244 us -> 634 us (2.60)
  blocking collectives: 93.6 us -> 557 us
  waiting for transfers between devices: 77.4 us -> 0.01 us
  between operations: 14.2 us -> 0.88 us
  local copies, waits for them, and re-layouts: 2.34 us -> 12.6 us
  starting transfers between devices: 0.01 us -> 8.76 us
    unnamed x2, blocking collectives: 42.8 us -> 505 us
    all_gather x1 -> x0, waiting for transfers between devices: 76.7 us -> none  [on_device(): lax.all_gather(latent_vectors, TOK, axis=0, tiled=True)]
    another operation x0 -> x1, local copies, waits for them, and re-layouts: none -> 11.5 us  [on_device(): jnp.stack([latent_vectors] * lax.axis_size(TOK))]
    all_to_all x0 -> x1, starting transfers between devices: none -> 8.76 us  [on_device(): lax.all_to_all(jnp.stack([latent_vectors] * lax.axis_size(TOK)), TOK, 0, 0)]
  transfers between devices with their start and end apart: 1 -> 1, of which waited for: 1 -> 0; matrix products, arithmetic and copies ran while one was open for 2% -> 0% of each run, Pallas kernels for 0% -> 0%
where the time goes in v1:
time: 634 us; the launch traced here: 633 us
  blocking collectives  557 us (88%)
  matrix products  52.4 us (8%)
  local copies, waits for them, and re-layouts  12.6 us (2%)
  starting transfers between devices  8.76 us (1%)
    unnamed x2, blocking collectives  505 us
    all_gather x4, blocking collectives, collected_together(): both, at, found = (lax.all_gather(jnp.concatenate(lines), axis), 0, {})  52 us
    dot_general x1, matrix products, on_device(): jnp.dot(gathered, unembedding_matrix, preferred_element_type=jnp.float32,...  51.2 us
  transfers between devices with their start and end apart: 1, of which 0 were waited for; matrix products, arithmetic and copies ran while one was open for 0% of the time, Pallas kernels for 0%

profile of v1, /device:TPU:2, one launch (start us, length us, event | category | flops | bytes accessed | tf_op | source)
XLA Modules:
  0.0 633.4 jit_solution(15765267473105432334)
XLA Ops:
  0.0 11.5 %stack.2 = f32[16,96,3584]{2,1,0:T(8,128)} broadcast(f32[96,3584]{1,0:T(8,128)} %param.6), dimensions={1,2} | broadcast | bytes 23396352 | tf_op jit(solution)/shard_map/stack | solution.py:71
  11.5 0.0 copy-start.3
  11.5 0.0 copy-start.4
  11.5 0.0 copy-start
  11.5 0.0 copy-start.1
  11.5 0.0 copy-start.2
  11.5 8.8 %all-to-all-start = ((f32[16,96,3584]{2,1,0:T(8,128)}), f32[16,96,3584]{2,1,0:T(8,128)}, u32[]{:S(2)}, u32[]{:S(2)}) async-start(f32[16,96,3584]{2,1,0:T(8,128)} %stack.2), calls=%async_computation | async-start | bytes 44040192 | tf_op jit(solution)/shard_map/all_to_all | solution.py:71
  20.3 0.0 copy-done.3
  20.3 0.2 reduce-window.7
  20.5 0.0 copy-done.4
  20.5 0.6 dynamic-slice
  21.8 0.0 copy-done
  21.8 0.0 copy-done.1
  21.8 0.2 convolution_bitcast_fusion.2
  22.0 0.2 convolution_bitcast_fusion.1
  22.2 0.2 dynamic-update-slice
  22.4 0.0 copy-done.2
  22.4 0.3 dynamic-update-slice.1
  22.7 493.0 %all-reduce = f32[1536]{0:T(1024)S(1)} all-reduce(f32[1536]{0:T(1024)S(1)} %dynamic-update-slice), channel_id=1, replica_groups=mesh['tok_0'=8,'tok_1'=2,'vocab_0'=4,'vocab_1'=4] {'tok_0','tok_1'}, use_global_device_ids=true, to_apply=%add | all-reduce | flops 1536 | bytes 12288
  515.7 12.1 %all-reduce.1 = s32[1536]{0:T(1024)S(1)} all-reduce(s32[1536]{0:T(1024)S(1)} %dynamic-update-slice.1), channel_id=1, replica_groups=mesh['tok_0'=8,'tok_1'=2,'vocab_0'=4,'vocab_1'=4] {'tok_0','tok_1'}, use_global_device_ids=true, to_apply=%add.1 | all-reduce | flops 1536 | bytes 12288
  527.8 0.0 all-to-all-done
  527.8 51.2 %fusion.65 = (f32[1536]{0:T(1024)S(1)}, f32[1536,594]{0,1:T(8,128)S(1)}) fusion(f32[1536]{0:T(1024)S(1)} %all-reduce, f32[1536,3584]{1,0:T(8,128)} %bitcast.3, f32[3584,594]{0,1:T(8,128)} %param.7), kind=kOutput, calls=%fused_computation.134 | convolution fusion | flops 39241633792 | bytes 34197504 | tf_op jit(solution)/shard_map/dot_general | solution.py:79
  579.1 0.9 exponential_reduce_fusion
  580.0 25.7 %all-gather.4 = f32[8,3,1536]{2,1,0:T(4,128)S(1)} all-gather(f32[1,3,1536]{2,1,0:T(4,128)S(1)} %maximum_bitcast_fusion), channel_id=2, replica_groups=mesh['tok_0'=8,'tok_1'=2,'vocab_0'=4,'vocab_1'=4] {'tok_0'}, dimensions={0}, use_global_device_ids=true | all-gather | bytes 165888 | tf_op jit(solution)/shard_map/all_gather | solution.py:20
  605.8 0.1 fusion.19
  605.9 1.8 all-gather.5
  607.9 12.4 %all-gather.6 = f32[4,3,1536]{2,1,0:T(4,128)S(1)} all-gather(f32[1,3,1536]{2,1,0:T(4,128)S(1)} %maximum_bitcast_fusion.2), channel_id=4, replica_groups=mesh['tok_0'=8,'tok_1'=2,'vocab_0'=4,'vocab_1'=4] {'vocab_0'}, dimensions={0}, use_global_device_ids=true | all-gather | bytes 92160 | tf_op jit(solution)/shard_map/all_gather | solution.py:20
  620.3 0.1 fusion.5
  620.4 12.0 %all-gather.7 = f32[4,3,1536]{2,1,0:T(4,128)S(1)} all-gather(f32[1,3,1536]{2,1,0:T(4,128)S(1)} %maximum_bitcast_fusion.3), channel_id=5, replica_groups=mesh['tok_0'=8,'tok_1'=2,'vocab_0'=4,'vocab_1'=4] {'vocab_1'}, dimensions={0}, use_global_device_ids=true | all-gather | bytes 92160 | tf_op jit(solution)/shard_map/all_gather | solution.py:20
  632.4 0.2 slice_reduce_fusion.3
  632.6 0.7 fusion
  (19 shorter events, 0.3 us)
Async XLA Ops:
  11.5 8.8 %copy-start.3 = (s32[1,4]{1,0:T(1,128)S(1)}, s32[1,4]{1,0:T(1,128)}, u32[]{:S(2)}) copy-start(s32[1,4]{1,0:T(1,128)} %param.9) | copy-start | bytes 52
  11.5 9.0 %copy-start.4 = (u32[256]{0:T(256)S(1)}, u32[256]{0:T(256)}, u32[]{:S(2)}) copy-start(u32[256]{0:T(256)} %constant.47) | copy-start | bytes 3076
  11.5 10.2 %copy-start = (f32[1024]{0:T(1024)S(1)}, f32[1024]{0:T(1024)}, u32[]{:S(2)}) copy-start(f32[1024]{0:T(1024)} %param.11) | copy-start | bytes 12292
  11.5 10.3 %copy-start.1 = (s32[1,4]{1,0:T(1,128)S(1)}, s32[1,4]{1,0:T(1,128)}, u32[]{:S(2)}) copy-start(s32[1,4]{1,0:T(1,128)} %param.10) | copy-start | bytes 52
  11.5 10.9 %copy-start.2 = (s32[96]{0:T(128)S(1)}, s32[96]{0:T(128)}, u32[]{:S(2)}) copy-start(s32[96]{0:T(128)} %param.8) | copy-start | bytes 1156
  11.5 516.3 %all-to-all-start = ((f32[16,96,3584]{2,1,0:T(8,128)}), f32[16,96,3584]{2,1,0:T(8,128)}, u32[]{:S(2)}, u32[]{:S(2)}) async-start(f32[16,96,3584]{2,1,0:T(8,128)} %stack.2), calls=%async_computation | async-start | bytes 44040192 | tf_op jit(solution)/shard_map/all_to_all | solution.py:71
